TPU v7x, 8 devices: a whole 2x2x1 slice. The times are simulated.
8 devices in a mesh: dp: 2 (over z, y), tp: 4 (over x, core).
Axes of the slice: x: 2, y: 2, z: 1, core: 2. Of those that a mesh axis runs over, the one named last changes fastest.
Arguments:
- tokens_in: bfloat16 [2, 256, 1664], P('dp'), parts along dimension 0
- ln_scale: bfloat16 [2, 1664], replicated
- w_query: bfloat16 [2, 1664, 1664], P(None, None, 'tp')
- w_key: bfloat16 [2, 1664, 1664], P(None, None, 'tp')
- w_value: bfloat16 [2, 1664, 1664], P(None, None, 'tp')
- q_scale: bfloat16 [2, 104], replicated
- k_scale: bfloat16 [2, 104], replicated
- w_out: bfloat16 [2, 1664, 1664], P(None, 'tp')
- b_out: bfloat16 [2, 1664], replicated
- w_up: bfloat16 [2, 1664, 8192], P(None, None, 'tp')
- b_up: bfloat16 [2, 8192], P(None, 'tp')
- w_down: bfloat16 [2, 8192, 1664], P(None, 'tp')
- b_down: bfloat16 [2, 1664], replicated
Outputs:
- output: bfloat16 [2, 256, 1664], P('dp'), parts along dimension 0
There are 2 independent parts. A program takes and returns all parts, laid end to end along the dimension named above; an argument that names none is the same for every part.
All inputs are finite; a program needn't handle non-finite values.
Results may differ from a plain program's by a relative error of at most 0.012433.
Values are sent between devices in bfloat16 or wider.
A program may use at most 1 GiB of HBM per device.

v0:
```python
import jax
import jax.numpy as jnp
from jax import lax
from jax.sharding import PartitionSpec as P

LN_EPS = 1e-6


def layer_norm(values, scale_vec):
    mean_val = jnp.mean(values, axis=-1, keepdims=True)
    centered = values - mean_val
    variance = jnp.mean(centered * centered, axis=-1, keepdims=True)
    return centered * lax.rsqrt(variance + LN_EPS) * scale_vec.astype(jnp.float32)


def local_branches(normed, n_images, seq_len, w_query, w_key, w_value, q_scale, k_scale, w_out, w_up, b_up, w_down):
    head_dim = q_scale.shape[0]
    local_heads = w_query.shape[1] // head_dim

    def project(weight):
        projected = jnp.dot(normed, weight, preferred_element_type=jnp.float32)
        return projected.reshape(n_images, seq_len, local_heads, head_dim)

    queries = layer_norm(project(w_query), q_scale).astype(jnp.bfloat16)
    keys_all = layer_norm(project(w_key), k_scale).astype(jnp.bfloat16)
    values_all = project(w_value).astype(jnp.bfloat16)
    scores = jnp.einsum("bqhd,bkhd->bhqk", queries, keys_all, preferred_element_type=jnp.float32) * head_dim ** -0.5
    attn_prob = jax.nn.softmax(scores, axis=-1).astype(jnp.bfloat16)
    mixed_val = jnp.einsum("bhqk,bkhd->bqhd", attn_prob, values_all, preferred_element_type=jnp.float32)
    mixed_val = mixed_val.astype(jnp.bfloat16).reshape(n_images * seq_len, local_heads * head_dim)
    attn_part = jnp.dot(mixed_val, w_out, preferred_element_type=jnp.float32)
    pre_act = jnp.dot(normed, w_up, preferred_element_type=jnp.float32) + b_up.astype(jnp.float32)
    activated = jax.nn.gelu(pre_act, approximate=True).astype(jnp.bfloat16)
    return attn_part + jnp.dot(activated, w_down, preferred_element_type=jnp.float32)


def solution(mesh):
    col_spec = P(None, None, "tp")
    row_spec = P(None, "tp", None)
    in_specs = (P("dp", None, None), P(), col_spec, col_spec, col_spec, P(), P(), row_spec, P(), col_spec, P(None, "tp"), row_spec, P())

    def per_device(tokens_in, ln_scale, w_query, w_key, w_value, q_scale, k_scale, w_out, b_out, w_up, b_up, w_down, b_down):
        n_images, seq_len, model_dim = tokens_in.shape
        n_tokens = n_images * seq_len
        current = tokens_in
        for layer_idx in range(w_query.shape[0]):
            residual = current.reshape(n_tokens, model_dim).astype(jnp.float32)
            normed = layer_norm(residual, ln_scale[layer_idx]).astype(jnp.bfloat16)
            part_sum = local_branches(normed, n_images, seq_len, w_query[layer_idx], w_key[layer_idx], w_value[layer_idx], q_scale[layer_idx], k_scale[layer_idx], w_out[layer_idx], w_up[layer_idx], b_up[layer_idx], w_down[layer_idx])
            reduced = lax.psum(part_sum.astype(jnp.bfloat16), "tp")
            summed = residual + b_out[layer_idx].astype(jnp.float32) + b_down[layer_idx].astype(jnp.float32) + reduced.astype(jnp.float32)
            current = summed.astype(jnp.bfloat16).reshape(n_images, seq_len, model_dim)
        return current

    return jax.shard_map(per_device, mesh=mesh, in_specs=in_specs, out_specs=P("dp", None, None), check_vma=False)
```

profile of v0, /device:TPU:0, one launch (start us, length us, event | category | flops | bytes accessed | tf_op | source)
XLA Modules:
  0.0 125.2 jit_solution(11892273309735252293)
XLA Ops:
  6.5 0.0 copy-start
  6.5 0.0 copy-start.2
  6.5 0.0 all-reduce.3.cloned.1.call-start
  6.5 1.4 %convert_reduce_fusion.1 = f32[256]{0:T(256)S(1)} fusion(bf16[1,256,1664]{2,1,0:T(8,128)(2,1)} %param.13), kind=kLoop, calls=%fused_computation.26 | loop fusion | flops 851712 | bytes 852992 | tf_op jit(solution)/shard_map/reduce_sum | solution.py:10
  8.0 1.5 %fusion.57 = f32[256]{0:T(256)S(1)} fusion(bf16[1,256,1664]{2,1,0:T(8,128)(2,1)} %param.13, f32[256]{0:T(256)S(1)} %broadcast_multiply_fusion.5), kind=kLoop, calls=%fused_computation.55 | loop fusion | flops 1703680 | bytes 854016 | tf_op jit(solution)/shard_map/reduce_sum | solution.py:12
  9.5 0.0 copy-done.2
  9.6 0.0 copy-done
  9.6 2.0 %fusion.72 = f32[256,416]{0,1:T(8,128)S(1)} fusion(bf16[2,1664,416]{1,2,0:T(8,128)(2,1)} %param.16, bf16[1,256,1664]{2,1,0:T(8,128)(2,1)S(1)} %copy-done, f32[1664]{0:T(1024)S(1)} %get-tuple-element.10, f32[256]{0:T(256)S(1)} %add_rsqrt_fusion.5, f32[256]{0:T(256)S(1)} %broadcast_multiply_fusion.5), kind=kOutput, calls=%fused_computation.70 | convolution fusion | flops 356548608 | bytes 2671104 | tf_op jit(solution)/shard_map/dot_general | solution.py:21
  11.7 0.0 copy-start.5
  11.7 0.0 copy-start.6
  11.7 2.0 %fusion.74 = f32[256,416]{0,1:T(8,128)S(1)} fusion(bf16[2,1664,416]{1,2,0:T(8,128)(2,1)} %param.15, bf16[1,256,1664]{2,1,0:T(8,128)(2,1)S(1)} %copy-done, f32[1664]{0:T(1024)S(1)} %get-tuple-element.10, f32[256]{0:T(256)S(1)} %add_rsqrt_fusion.5, f32[256]{0:T(256)S(1)} %broadcast_multiply_fusion.5), kind=kOutput, calls=%fused_computation.72 | convolution fusion | flops 356548608 | bytes 2671104 | tf_op jit(solution)/shard_map/dot_general | solution.py:21
  13.8 0.1 multiply_reduce_fusion.2
  13.9 0.1 multiply_reduce_fusion.3
  13.9 0.0 copy-done.5
  14.0 0.0 copy-done.6
  14.0 0.4 convolution_multiply_fusion.1
  14.4 0.6 fusion.138
  15.0 0.0 copy-start.1
  15.0 3.1 %fusion.137 = (bf16[1,1664,416]{1,2,0:T(8,128)(2,1)}, bf16[1,1664,416]{1,2,0:T(8,128)(2,1)S(1)}) fusion(bf16[2,1664,416]{1,2,0:T(8,128)(2,1)} %param.17), kind=kLoop, calls=%fused_computation.154 | loop fusion | bytes 5537792 | tf_op jit(solution)/shard_map/slice | solution.py:49
  18.1 0.0 copy-done.1
  18.1 1.1 convolution_convert_fusion.2
  19.2 9.1 %fusion.6 = f32[256,1664]{1,0:T(8,128)S(1)} fusion(bf16[2,2048,1664]{2,1,0:T(8,128)(2,1)} %param.24, bf16[2,1664,2048]{2,1,0:T(8,128)(2,1)} %param.22, f32[2048]{0:T(1024)S(1)} %bitcast.151, bf16[1,256,1664]{2,1,0:T(8,128)(2,1)S(1)} %copy-done, f32[1664]{0:T(1024)S(1)} %get-tuple-element.10, f32[256]{0:T(256)S(1)} %add_rsqrt_fusion.5, ...), kind=kOutput, calls=%fused_computation.6 | convolution fusion | flops 3497033728 | bytes 16204288 | tf_op jit(solution)/shard_map/dot_general | solution.py:34
  28.3 0.0 copy-start.3
  28.3 0.0 copy-start.4
  28.3 2.9 %fusion.20 = bf16[256,1664]{1,0:T(8,128)(2,1)} fusion(f32[256,1664]{1,0:T(8,128)S(1)} %fusion.6, bf16[256,416]{0,1:T(8,128)(2,1)S(1)} %bitcast.148, bf16[2,416,1664]{2,1,0:T(8,128)(2,1)} %param.20), kind=kOutput, calls=%fused_computation.20 | convolution fusion | flops 355270656 | bytes 4153344 | tf_op jit(solution)/shard_map/dot_general | solution.py:31
  31.2 0.0 all-reduce.3.cloned.1.call-update
  31.2 0.2 all-reduce.5.cloned.1.call-start
  31.5 0.0 copy-done.3
  31.5 0.0 copy-done.4
  31.5 0.1 convert_reduce_fusion.3
  31.6 32.5 %all-reduce.3.cloned.1.call-done = bf16[256,1664]{1,0:T(8,128)(2,1)} async-done(((bf16[256,1664]{1,0:T(8,128)(2,1)}), bf16[256,1664]{1,0:T(8,128)(2,1)}) %all-reduce.3.cloned.1.call-update) | async-done | bytes 851984 | tf_op jit(solution)/shard_map/psum | solution.py:50
  64.0 0.0 copy-start.7
  64.0 1.8 %convert_reduce_fusion = (f32[256]{0:T(256)S(1)}, bf16[256,1664]{1,0:T(8,128)(2,1)S(1)}) fusion(bf16[256,1664]{1,0:T(8,128)(2,1)} %all-reduce.3.cloned.1.call-done, f32[1664]{0:T(1024)S(1)} %get-tuple-element.8, f32[1664]{0:T(1024)S(1)} %get-tuple-element.25, bf16[1,256,1664]{2,1,0:T(8,128)(2,1)S(1)} %copy-done), kind=kLoop, calls=%fused_computation.23 | loop fusion | flops 3407616 | bytes 2570240 | tf_op jit(solution)/shard_map/reduce_sum | solution.py:10
  65.8 0.4 fusion.50
  66.2 0.0 copy-done.7
  66.2 0.0 copy-start.8
  66.2 0.7 fusion.69
  66.9 1.1 copy-done.8
  68.0 0.7 fusion.67
  68.7 0.1 multiply_reduce_fusion.1
  68.9 0.1 multiply_reduce_fusion
  68.9 1.4 %convolution_multiply_fusion = f32[4,256,256]{1,2,0:T(8,128)} fusion(f32[256,4,104]{0,2,1:T(8,128)S(1)} %bitcast.140, f32[256,4,104]{0,2,1:T(8,128)S(1)} %bitcast.144, f32[104]{0:T(128)S(1)} %get-tuple-element.19, f32[256,4]{0,1:T(4,128)S(1)} %add_rsqrt_fusion, f32[256,4]{0,1:T(4,128)S(1)} %broadcast_multiply_fusion, f32[104]{0:T(128)S(1)} %get-tuple-element.24, ...), kind=kOutput, calls=%fused_computation.82 | convolution fusion | flops 55640064 | bytes 1917760 | tf_op jit(solution)/shard_map/bqhd,bkhd->bhqk/dot_general | solution.py:27
  70.3 0.6 fusion.139
  70.9 9.1 %fusion.2 = f32[256,1664]{1,0:T(8,128)S(1)} fusion(bf16[2,2048,1664]{2,1,0:T(8,128)(2,1)} %param.24, bf16[2,1664,2048]{2,1,0:T(8,128)(2,1)} %param.22, f32[2048]{0:T(1024)S(1)} %bitcast.150, bf16[256,1664]{1,0:T(8,128)(2,1)S(1)} %get-tuple-element.12, f32[1664]{0:T(1024)S(1)} %get-tuple-element.9, f32[256]{0:T(256)S(1)} %add_rsqrt_fusion.4, ...), kind=kOutput, calls=%fused_computation.2 | convolution fusion | flops 3497033728 | bytes 16204288 | tf_op jit(solution)/shard_map/dot_general | solution.py:34
  80.0 3.0 %convolution_convert_fusion = bf16[4,104,256]{2,1,0:T(8,128)(2,1)S(1)} fusion(bf16[4,104,1664]{2,1,0:T(8,128)(2,1)} %bitcast.146, f32[4,256]{1,0:T(4,128)S(1)} %fusion.139, f32[4,256,256]{1,2,0:T(8,128)} %convolution_multiply_fusion, bf16[256,1664]{1,0:T(8,128)(2,1)S(1)} %get-tuple-element.12, f32[1664]{0:T(1024)S(1)} %get-tuple-element.9, ...), kind=kOutput, calls=%fused_computation.84 | convolution fusion | flops 412075264 | bytes 3510784 | tf_op jit(solution)/shard_map/bhqk,bkhd->bqhd/dot_general | solution.py:29
  83.0 2.9 %fusion.21 = bf16[256,1664]{1,0:T(8,128)(2,1)} fusion(f32[256,1664]{1,0:T(8,128)S(1)} %fusion.2, bf16[256,416]{0,1:T(8,128)(2,1)S(1)} %bitcast.149, bf16[2,416,1664]{2,1,0:T(8,128)(2,1)} %param.20), kind=kOutput, calls=%fused_computation.21 | convolution fusion | flops 355270656 | bytes 4153344 | tf_op jit(solution)/shard_map/dot_general | solution.py:31
  86.0 0.0 all-reduce.5.cloned.1.call-update
  86.0 30.0 %all-reduce.5.cloned.1.call-done = bf16[256,1664]{1,0:T(8,128)(2,1)} async-done(((bf16[256,1664]{1,0:T(8,128)(2,1)}), bf16[256,1664]{1,0:T(8,128)(2,1)}) %all-reduce.5.cloned.1.call-update) | async-done | bytes 851984 | tf_op jit(solution)/shard_map/psum | solution.py:50
  116.0 2.4 %fusion.84 = bf16[1,256,1664]{2,1,0:T(8,128)(2,1)} fusion(bf16[256,1664]{1,0:T(8,128)(2,1)} %all-reduce.5.cloned.1.call-done, bf16[256,1664]{1,0:T(8,128)(2,1)S(1)} %get-tuple-element.12, f32[1664]{0:T(1024)S(1)} %get-tuple-element.7, f32[1664]{0:T(1024)S(1)} %get-tuple-element.26), kind=kLoop, calls=%fused_computation.90 | loop fusion | flops 2555904 | bytes 2569216 | tf_op jit(solution)/shard_map/reshape | solution.py:52
  (18 shorter events, 0.3 us)
Async XLA Ops:
  6.5 3.0 %copy-start = (bf16[1,256,1664]{2,1,0:T(8,128)(2,1)S(1)}, bf16[1,256,1664]{2,1,0:T(8,128)(2,1)}, u32[]{:S(2)}) copy-start(bf16[1,256,1664]{2,1,0:T(8,128)(2,1)} %param.13) | copy-start | bytes 2555908
  6.5 3.0 %copy-start.2 = (bf16[2,1664]{1,0:T(2,128)(2,1)S(1)}, bf16[2,1664]{1,0:T(2,128)(2,1)}, u32[]{:S(2)}) copy-start(bf16[2,1664]{1,0:T(2,128)(2,1)} %param.14) | copy-start | bytes 19972
  6.5 57.5 %all-reduce.3.cloned.1.call-start = ((), (), s32[]{:S(2)}) async-start(), calls=%async_computation | async-start | bytes 1703936 | tf_op jit(solution)/shard_map/psum | solution.py:50
  11.7 2.3 %copy-start.5 = (bf16[2,104]{1,0:T(2,128)(2,1)S(1)}, bf16[2,104]{1,0:T(2,128)(2,1)}, u32[]{:S(2)}) copy-start(bf16[2,104]{1,0:T(2,128)(2,1)} %param.19) | copy-start | bytes 1252
  11.7 2.3 %copy-start.6 = (bf16[2,104]{1,0:T(2,128)(2,1)S(1)}, bf16[2,104]{1,0:T(2,128)(2,1)}, u32[]{:S(2)}) copy-start(bf16[2,104]{1,0:T(2,128)(2,1)} %param.18) | copy-start | bytes 1252
  15.0 3.1 %copy-start.1 = (bf16[2,2048]{1,0:T(2,128)(2,1)S(1)}, bf16[2,2048]{1,0:T(2,128)(2,1)}, u32[]{:S(2)}) copy-start(bf16[2,2048]{1,0:T(2,128)(2,1)} %param.23) | copy-start | bytes 24580
  28.3 3.2 %copy-start.3 = (bf16[2,1664]{1,0:T(2,128)(2,1)S(1)}, bf16[2,1664]{1,0:T(2,128)(2,1)}, u32[]{:S(2)}) copy-start(bf16[2,1664]{1,0:T(2,128)(2,1)} %param.25) | copy-start | bytes 19972
  28.3 3.2 %copy-start.4 = (bf16[2,1664]{1,0:T(2,128)(2,1)S(1)}, bf16[2,1664]{1,0:T(2,128)(2,1)}, u32[]{:S(2)}) copy-start(bf16[2,1664]{1,0:T(2,128)(2,1)} %param.21) | copy-start | bytes 19972
  31.2 84.7 %all-reduce.5.cloned.1.call-start = ((), (), s32[]{:S(2)}) async-start(), calls=%async_computation.1 | async-start | bytes 1703936 | tf_op jit(solution)/shard_map/psum | solution.py:50
  64.0 2.1 %copy-start.7 = (bf16[2,1664,416]{1,2,0:T(8,128)(2,1)S(1)}, bf16[2,1664,416]{1,2,0:T(8,128)(2,1)}, u32[]{:S(2)}) copy-start(bf16[2,1664,416]{1,2,0:T(8,128)(2,1)} %param.15) | copy-start | bytes 8306692
  66.2 1.8 %copy-start.8 = (bf16[2,1664,416]{1,2,0:T(8,128)(2,1)S(1)}, bf16[2,1664,416]{1,2,0:T(8,128)(2,1)}, u32[]{:S(2)}) copy-start(bf16[2,1664,416]{1,2,0:T(8,128)(2,1)} %param.16) | copy-start | bytes 8306692
Sparse Core Ops, SparseCore 0:
  31.3 32.6 all-reduce.2
  86.1 29.8 all-reduce.4
where the time goes:
time: 126 us; the launch traced here: 125 us
  waiting for transfers between devices  62.5 us (50%)
  matrix products  36.5 us (29%)
  between operations  13.7 us (11%)
  other arithmetic  8.05 us (6%)
  local copies, waits for them, and re-layouts  4.19 us (3%)
    psum x2, waiting for transfers between devices, per_device(): reduced = lax.psum(part_sum.astype(jnp.bfloat16), 'tp')  62.5 us
    dot_general x2, matrix products, local_branches(): jnp.dot(activated, w_down, preferred_element_type=jnp.float32)  18.1 us
    dot_general x2, matrix products, local_branches(): attn_part = jnp.dot(mixed_val, w_out, preferred_element_type=jnp.float32)  5.83 us
    dot_general x4, matrix products, project(): projected = jnp.dot(normed, weight, preferred_element_type=jnp.float32)  5.46 us
    dot_general x2, matrix products, local_branches(): jnp.einsum('bhqk,bkhd->bqhd', attn_prob, values_all, preferred_element_ty...  4.09 us
    reduce_sum x6, other arithmetic, layer_norm(): mean_val = jnp.mean(values, axis=-1, keepdims=True)  3.35 us
    slice x1, local copies, waits for them, and re-layouts, per_device(): w_value[layer_idx]  3.07 us
  transfers between devices with their start and end apart: 2, of which 2 were waited for; matrix products, arithmetic and copies ran while one was open for 0% of the time, Pallas kernels for 0%

commit v1 on v0

v1 whole, which is shorter than its diff:
```python
import functools

import jax
import jax.numpy as jnp
from jax import lax
from jax.experimental import pallas as pl
from jax.experimental.pallas import tpu as pltpu
from jax.sharding import PartitionSpec as P

LN_EPS = 1e-6
MESH = pl.DeviceIdType.MESH
F32 = jnp.float32
BF16 = jnp.bfloat16

T = 256
D = 1664
HD = 104
NH = 4
HW = NH * HD
FF = 2048
CH = 128
OWN = CH // 2
WIN = 256
WIN0 = (0, 0, 128, 256)
OFF = (0, 104, 80, 56)
COLS = ((0, 512), (512, 512), (1024, 640))
UPB = ((0, 512), (512, 512), (1024, 512), (1536, 512))
NB = len(COLS)


def kernel(x_hbm, lns_ref, wq_hbm, wk_hbm, wv_hbm, qs_ref, ks_ref, wo_hbm, bo_ref, wu_hbm, bu_ref, wd_hbm, bd_ref,
           out_hbm,
           x_s, wq_s, wk_s, wv_s, wo_s, wu_s, wd_s,
           h_s, proj_s, q4_s, k4_s, v4_s, o_s, act_s, acc_s,
           dsend, drecv, xsend, xrecv, y_s,
           wsem, iosem, dss, drs, xss, xrs, fss, frs):
    tp = lax.axis_index("tp")
    core = lax.rem(tp, 2)
    sib = tp + 1 - 2 * core
    cross = lax.rem(tp + 2, 4)

    xcopy = pltpu.make_async_copy(x_hbm.at[0], x_s, iosem.at[0])
    xcopy.start()
    wcopies = {}
    nsem = [0]

    def wcopy(name, l, src, dst):
        wcopies[(name, l)] = pltpu.make_async_copy(src, dst, wsem.at[nsem[0]])
        nsem[0] += 1

    for l in range(2):
        wcopy("k", l, wk_hbm.at[l], wk_s.at[l])
        wcopy("v", l, wv_hbm.at[l], wv_s.at[l])
        wcopy("q", l, wq_hbm.at[l], wq_s.at[l])
        for i, (n0, nn) in enumerate(UPB):
            wcopy(("u", i), l, wu_hbm.at[l, :, pl.ds(n0, nn)], wu_s.at[l, :, pl.ds(n0, nn)])
        for i, (n0, nn) in enumerate(COLS):
            wcopy(("o", i), l, wo_hbm.at[l, :, pl.ds(n0, nn)], wo_s.at[l, :, pl.ds(n0, nn)])
            wcopy(("d", i), l, wd_hbm.at[l, :, pl.ds(n0, nn)], wd_s.at[l, :, pl.ds(n0, nn)])
    for (name, l), cp in wcopies.items():
        if l == 0:
            cp.start()
    waited = set()

    def need(name, l):
        if (name, l) not in waited:
            waited.add((name, l))
            wcopies[(name, l)].wait()

    barrier = pltpu.get_barrier_semaphore()
    for peer in (sib, cross):
        pl.semaphore_signal(barrier, inc=1, device_id={"tp": peer}, device_id_type=MESH)

    lane = lax.broadcasted_iota(jnp.int32, (8, WIN), 1)
    masks = [(lane >= OFF[i]) & (lane < OFF[i] + HD) for i in range(NH)]

    def mask_of(i, rows):
        lane_r = lax.broadcasted_iota(jnp.int32, (rows, WIN), 1)
        return (lane_r >= OFF[i]) & (lane_r < OFF[i] + HD)

    def gain_windows(ref, l):
        g = ref[l : l + 1, :].astype(F32)
        g = jnp.concatenate([g, jnp.zeros((1, WIN - HD), F32)], axis=1)
        g8 = jnp.broadcast_to(g, (8, WIN))
        return [(pltpu.roll(g8, OFF[i], 1) if OFF[i] else g8)[0:1, :] for i in range(NH)]

    def ln_rows(src, l, rows):
        v = src[rows, :].astype(F32)
        mean = jnp.sum(v, axis=1, keepdims=True) * (1.0 / D)
        cen = v - mean
        var = jnp.sum(cen * cen, axis=1, keepdims=True) * (1.0 / D)
        g = lns_ref[l : l + 1, :].astype(F32)
        h_s[rows, :] = (cen * lax.rsqrt(var + LN_EPS) * g).astype(BF16)

    def head_norm(dst, gains, rows, n):
        for i in range(NH):
            w = proj_s[rows, pl.ds(WIN0[i], WIN)]
            m = mask_of(i, n)
            w = jnp.where(m, w, 0.0)
            mean = jnp.sum(w, axis=1, keepdims=True) * (1.0 / HD)
            cen = jnp.where(m, w - mean, 0.0)
            var = jnp.sum(cen * cen, axis=1, keepdims=True) * (1.0 / HD)
            dst[i, rows, :] = (cen * lax.rsqrt(var + LN_EPS) * gains[i]).astype(BF16)

    def project(w_s, l, rows):
        proj_s[rows, pl.ds(0, HW)] = jnp.dot(h_s[rows, :], w_s[l], preferred_element_type=F32)

    def do_k(l, rows, n, gk):
        need("k", l)
        project(wk_s, l, rows)
        head_norm(k4_s, gk, rows, n)

    def do_v(l, rows, n):
        need("v", l)
        project(wv_s, l, rows)
        for i in range(NH):
            w = proj_s[rows, pl.ds(WIN0[i], WIN)]
            v4_s[i, rows, :] = jnp.where(mask_of(i, n), w, 0.0).astype(BF16)

    def do_q(l, rows, n, gq):
        need("q", l)
        project(wq_s, l, rows)
        head_norm(q4_s, gq, rows, n)

    def attend(rows):
        os = []
        for i in range(NH):
            s = lax.dot_general(q4_s[i, rows, :], k4_s[i], (((1,), (1,)), ((), ())), preferred_element_type=F32)
            s = s * (HD ** -0.5)
            e = jnp.exp(s - jnp.max(s, axis=1, keepdims=True))
            p = (e * (1.0 / jnp.sum(e, axis=1, keepdims=True))).astype(BF16)
            os.append(jnp.dot(p, v4_s[i], preferred_element_type=F32))
        lo = [o[:, 0:128] for o in os]
        hi = [o[:, 128:256] for o in os]
        o_s[rows, 0:128] = (lo[0] + lo[1]).astype(BF16)
        o_s[rows, 128:256] = (hi[1] + lo[2]).astype(BF16)
        o_s[rows, 256:384] = (hi[2] + lo[3]).astype(BF16)
        o_s[rows, 384:512] = hi[3].astype(BF16)

    def do_up(l, rows):
        for i, (n0, nn) in enumerate(UPB):
            need(("u", i), l)
            z = jnp.dot(h_s[rows, :], wu_s[l, :, pl.ds(n0, nn)], preferred_element_type=F32)
            z = z + bu_ref[l : l + 1, pl.ds(n0, nn)].astype(F32)
            t = jnp.tanh(z * (0.7978845608028654 + (0.7978845608028654 * 0.044715) * (z * z)))
            act_s[rows, pl.ds(n0, nn)] = (0.5 * z * (1.0 + t)).astype(BF16)

    def mlp_block(l, c, rows, b):
        n0, nn = COLS[b]
        need(("d", b), l)
        return jnp.dot(act_s[rows, :], wd_s[l, :, pl.ds(n0, nn)], preferred_element_type=F32)

    def attn_block(l, c, rows, b):
        n0, nn = COLS[b]
        need(("o", b), l)
        return jnp.dot(o_s[rows, pl.ds(0, HW)], wo_s[l, :, pl.ds(n0, nn)], preferred_element_type=F32)

    own_off = pl.multiple_of(core * OWN, OWN)
    sib_off = pl.multiple_of((1 - core) * OWN, OWN)

    def d_rdma(l, c, b):
        n0, nn = COLS[b]
        return pltpu.make_async_remote_copy(
            src_ref=dsend.at[l, c, :, pl.ds(n0, nn)], dst_ref=drecv.at[l, c, :, pl.ds(n0, nn)],
            send_sem=dss.at[l, c, b], recv_sem=drs.at[l, c, b], device_id={"tp": sib}, device_id_type=MESH)

    def x_rdma(l, c, b):
        n0, nn = COLS[b]
        return pltpu.make_async_remote_copy(
            src_ref=xsend.at[l, c, :, pl.ds(n0, nn)], dst_ref=xrecv.at[l, c, :, pl.ds(n0, nn)],
            send_sem=xss.at[l, c, b], recv_sem=xrs.at[l, c, b], device_id={"tp": cross}, device_id_type=MESH)

    def f_rdma(l, c, b):
        n0, nn = COLS[b]
        view = y_s.at[l, pl.ds(pl.multiple_of(c * CH + core * OWN, OWN), OWN), pl.ds(n0, nn)]
        return pltpu.make_async_remote_copy(
            src_ref=view, dst_ref=view,
            send_sem=fss.at[l, c, b], recv_sem=frs.at[l, c, b], device_id={"tp": sib}, device_id_type=MESH)

    def emit_block(l, c, b, part):
        n0, nn = COLS[b]
        acc_s[c, :, pl.ds(n0, nn)] = part
        dsend[l, c, :, pl.ds(n0, nn)] = acc_s[c, pl.ds(sib_off, OWN), pl.ds(n0, nn)].astype(BF16)
        d_rdma(l, c, b).start()

    def cross_block(l, c, b):
        n0, nn = COLS[b]
        d_rdma(l, c, b).wait_recv()
        s = acc_s[c, pl.ds(own_off, OWN), pl.ds(n0, nn)] + drecv[l, c, :, pl.ds(n0, nn)].astype(F32)
        xsend[l, c, :, pl.ds(n0, nn)] = s.astype(BF16)
        x_rdma(l, c, b).start()

    def finish_block(l, c, b):
        n0, nn = COLS[b]
        x_rdma(l, c, b).wait_recv()
        r = pl.ds(pl.multiple_of(c * CH + core * OWN, OWN), OWN)
        res = x_s[r, pl.ds(n0, nn)] if l == 0 else y_s[0, r, pl.ds(n0, nn)]
        base = res.astype(F32) + bo_ref[l : l + 1, pl.ds(n0, nn)].astype(F32) + bd_ref[l : l + 1, pl.ds(n0, nn)].astype(F32)
        both = xsend[l, c, :, pl.ds(n0, nn)].astype(F32) + xrecv[l, c, :, pl.ds(n0, nn)].astype(F32)
        y_s[l, r, pl.ds(n0, nn)] = (base + both).astype(BF16)
        f_rdma(l, c, b).start()

    rows = [pl.ds(0, CH), pl.ds(CH, CH)]
    proj_s[:, pl.ds(HW, 512 - HW)] = jnp.zeros((T, 512 - HW), F32)

    gk = gain_windows(ks_ref, 0)
    gq = gain_windows(qs_ref, 0)
    xcopy.wait()
    ln_rows(x_s, 0, rows[0])
    ln_rows(x_s, 0, rows[1])
    do_k(0, pl.ds(0, T), T, gk)
    do_v(0, pl.ds(0, T), T)
    do_q(0, rows[0], CH, gq)
    attend(rows[0])
    do_up(0, rows[0])
    pl.semaphore_wait(barrier, 2)
    for b in range(NB):
        emit_block(0, 0, b, mlp_block(0, 0, rows[0], b) + attn_block(0, 0, rows[0], b))
        if b >= 1:
            cross_block(0, 0, b - 1)
    for (name, l), cp in wcopies.items():
        if l == 1:
            cp.start()
    do_q(0, rows[1], CH, gq)
    cross_block(0, 0, NB - 1)
    attend(rows[1])
    do_up(0, rows[1])
    for b in range(NB):
        emit_block(0, 1, b, mlp_block(0, 1, rows[1], b) + attn_block(0, 1, rows[1], b))
        if b >= 1:
            cross_block(0, 1, b - 1)
    gk = gain_windows(ks_ref, 1)
    gq = gain_windows(qs_ref, 1)
    cross_block(0, 1, NB - 1)

    for b in range(NB):
        finish_block(0, 0, b)
    for b in range(NB):
        f_rdma(0, 0, b).wait_recv()
    y0 = y_s.at[0]
    ln_rows(y0, 1, rows[0])
    do_k(1, rows[0], CH, gk)
    do_v(1, rows[0], CH)
    do_q(1, rows[0], CH, gq)
    do_up(1, rows[0])
    for b in range(NB):
        acc_s[0, :, pl.ds(*COLS[b])] = mlp_block(1, 0, rows[0], b)
    for b in range(NB):
        finish_block(0, 1, b)
    for b in range(NB):
        f_rdma(0, 1, b).wait_recv()
    ln_rows(y0, 1, rows[1])
    do_k(1, rows[1], CH, gk)
    do_v(1, rows[1], CH)
    attend(rows[0])
    for b in range(NB):
        emit_block(1, 0, b, acc_s[0, :, pl.ds(*COLS[b])] + attn_block(1, 0, rows[0], b))
        if b >= 1:
            cross_block(1, 0, b - 1)
    do_q(1, rows[1], CH, gq)
    cross_block(1, 0, NB - 1)
    attend(rows[1])
    do_up(1, rows[1])
    for b in range(NB):
        emit_block(1, 1, b, mlp_block(1, 1, rows[1], b) + attn_block(1, 1, rows[1], b))
        if b >= 1:
            cross_block(1, 1, b - 1)
    cross_block(1, 1, NB - 1)

    def out_own(c):
        r = pl.ds(pl.multiple_of(c * CH + core * OWN, OWN), OWN)
        return pltpu.make_async_copy(y_s.at[1, r], out_hbm.at[0, r], iosem.at[1 + 2 * c])

    def out_sib(c):
        r = pl.ds(pl.multiple_of(c * CH + (1 - core) * OWN, OWN), OWN)
        return pltpu.make_async_copy(y_s.at[1, r], out_hbm.at[0, r], iosem.at[2 + 2 * c])

    for c in range(2):
        for b in range(NB):
            finish_block(1, c, b)
        out_own(c).start()
        for b in range(NB):
            f_rdma(1, c, b).wait_recv()
        out_sib(c).start()
    for l in range(2):
        for c in range(2):
            for b in range(NB):
                d_rdma(l, c, b).wait_send()
                x_rdma(l, c, b).wait_send()
                f_rdma(l, c, b).wait_send()
    for c in range(2):
        out_own(c).wait()
        out_sib(c).wait()


def solution(mesh):
    col_spec = P(None, None, "tp")
    row_spec = P(None, "tp", None)
    in_specs = (P("dp", None, None), P(), col_spec, col_spec, col_spec, P(), P(), row_spec, P(), col_spec, P(None, "tp"), row_spec, P())
    any_spec = pl.BlockSpec(memory_space=pl.ANY)
    vmem_spec = pl.BlockSpec(memory_space=pltpu.VMEM)
    nw = 2 * (3 + len(UPB) + 2 * NB)
    call = pl.pallas_call(
        kernel,
        out_shape=jax.ShapeDtypeStruct((1, T, D), BF16),
        in_specs=[any_spec, vmem_spec, any_spec, any_spec, any_spec, vmem_spec, vmem_spec, any_spec, vmem_spec, any_spec, vmem_spec, any_spec, vmem_spec],
        out_specs=any_spec,
        scratch_shapes=[
            pltpu.VMEM((T, D), BF16),
            pltpu.VMEM((2, D, HW), BF16),
            pltpu.VMEM((2, D, HW), BF16),
            pltpu.VMEM((2, D, HW), BF16),
            pltpu.VMEM((2, HW, D), BF16),
            pltpu.VMEM((2, D, FF), BF16),
            pltpu.VMEM((2, FF, D), BF16),
            pltpu.VMEM((T, D), BF16),
            pltpu.VMEM((T, 512), F32),
            pltpu.VMEM((NH, T, WIN), BF16),
            pltpu.VMEM((NH, T, WIN), BF16),
            pltpu.VMEM((NH, T, WIN), BF16),
            pltpu.VMEM((T, 512), BF16),
            pltpu.VMEM((T, FF), BF16),
            pltpu.VMEM((2, CH, D), F32),
            pltpu.VMEM((2, 2, OWN, D), BF16),
            pltpu.VMEM((2, 2, OWN, D), BF16),
            pltpu.VMEM((2, 2, OWN, D), BF16),
            pltpu.VMEM((2, 2, OWN, D), BF16),
            pltpu.VMEM((2, T, D), BF16),
            pltpu.SemaphoreType.DMA((nw,)),
            pltpu.SemaphoreType.DMA((5,)),
            pltpu.SemaphoreType.DMA((2, 2, NB)),
            pltpu.SemaphoreType.DMA((2, 2, NB)),
            pltpu.SemaphoreType.DMA((2, 2, NB)),
            pltpu.SemaphoreType.DMA((2, 2, NB)),
            pltpu.SemaphoreType.DMA((2, 2, NB)),
            pltpu.SemaphoreType.DMA((2, 2, NB)),
        ],
        compiler_params=pltpu.CompilerParams(collective_id=0, has_side_effects=True, vmem_limit_bytes=62 * 1024 * 1024),
        name="vit_pair",
    )

    def per_device(*args):
        return call(*args)

    return jax.shard_map(per_device, mesh=mesh, in_specs=in_specs, out_specs=P("dp", None, None), check_vma=False)
```

time: 126 us -> 68.1 us (0.54)
  waiting for transfers between devices: 62.5 us -> 0 us
  Pallas kernels: 0 us -> 51.1 us
  matrix products: 36.5 us -> 0 us
  between operations: 13.7 us -> 0.01 us
  local copies, waits for them, and re-layouts: 4.19 us -> 16.6 us
  other arithmetic: 8.05 us -> 0 us
    psum x2 -> x0, waiting for transfers between devices: 62.5 us -> none  [per_device(): reduced = lax.psum(part_sum.astype(jnp.bfloat16), 'tp')]
    pallas_call x0 -> x1, Pallas kernels: none -> 51.1 us  [per_device(): return call(*args)]
    dot_general x12 -> x0, matrix products: 35.3 us -> none  [the longest x2 18.1 us: local_branches(): jnp.dot(activated, w_down, preferred_element_type=jnp.float32)]
    unnamed x18 -> x6, local copies, waits for them, and re-layouts: 1.12 us -> 16.6 us
    reduce_sum x12 -> x0, other arithmetic: 5.48 us -> none  [the longest x6 3.35 us: layer_norm(): mean_val = jnp.mean(values, axis=-1, keepdims=True)]
    slice x1 -> x0, local copies, waits for them, and re-layouts: 3.07 us -> none  [per_device(): w_value[layer_idx]]
    reshape x1 -> x0, other arithmetic: 2.36 us -> none  [per_device(): current = summed.astype(jnp.bfloat16).reshape(n_images, seq_len, model_dim)]
  transfers between devices with their start and end apart: 2 -> 0, of which waited for: 2 -> 0; matrix products, arithmetic and copies ran while one was open for 0% -> 0% of each run, Pallas kernels for 0% -> 0%
where the time goes in v1:
time: 68.1 us; the launch traced here: 67.7 us
  Pallas kernels  51.1 us (75%)
  local copies, waits for them, and re-layouts  16.6 us (24%)
    pallas_call x1, Pallas kernels, per_device(): return call(*args)  51.1 us
    unnamed x6, local copies, waits for them, and re-layouts  16.6 us

profile of v1, /device:TPU:0, one launch (start us, length us, event | category | flops | bytes accessed | tf_op | source)
XLA Modules:
  0.0 67.7 jit_solution(18117688048596673264)
XLA Ops:
  0.0 0.0 copy-start
  0.0 5.5 %copy.14.wq_hbm = bf16[2,1664,416]{2,1,0:T(8,128)(2,1)} copy(bf16[2,1664,416]{1,2,0:T(8,128)(2,1)} %param.15) | data formatting | bytes 5537792 | tf_op args[2]
  5.5 0.0 copy-done
  5.5 3.6 %copy.15.wk_hbm = bf16[2,1664,416]{2,1,0:T(8,128)(2,1)} copy(bf16[2,1664,416]{1,2,0:T(8,128)(2,1)S(1)} %copy-done) | data formatting | bytes 5537792 | tf_op args[3]
  9.1 5.3 %copy.16.wv_hbm = bf16[2,1664,416]{2,1,0:T(8,128)(2,1)} copy(bf16[2,1664,416]{1,2,0:T(8,128)(2,1)} %param.17) | data formatting | bytes 5537792 | tf_op args[4]
  14.5 51.1 %vit_pair.1 = bf16[1,256,1664]{2,1,0:T(8,128)(2,1)} custom-call(bf16[1,256,1664]{2,1,0:T(8,128)(2,1)} %x_hbm.1, bf16[2,1664]{1,0:T(2,128)(2,1)} %lns_ref.1, bf16[2,1664,416]{2,1,0:T(8,128)(2,1)} %copy.14.wq_hbm, bf16[2,1664,416]{2,1,0:T(8,128)(2,1)} %copy.15.wk_hbm, bf16[2,1664,416]{2,1,0:T(8,128)(2,1)} %copy.16.wv_hbm, bf16[2,104]{1,0:T(2,128)(2,1)} %qs_ref.1, ...), custom_call_target="tpu_custom_call" | custom-call | tf_op jit(solution)/shard_map/vit_pair/pallas_call | solution.py:343
  65.6 2.1 %copy.18 = bf16[1,256,1664]{2,1,0:T(8,128)(2,1)} copy(bf16[1,256,1664]{2,1,0:T(8,128)(2,1)} %vit_pair.1) | data formatting | bytes 1703936
Async XLA Ops:
  0.0 5.5 %copy-start = (bf16[2,1664,416]{1,2,0:T(8,128)(2,1)S(1)}, bf16[2,1664,416]{1,2,0:T(8,128)(2,1)}, u32[]{:S(2)}) copy-start(bf16[2,1664,416]{1,2,0:T(8,128)(2,1)} %param.16) | copy-start | bytes 8306692

commit v2 on v1

--- a/solution.py
+++ b/solution.py
@@ -20,9 +20,6 @@
 FF = 2048
 CH = 128
 OWN = CH // 2
-WIN = 256
-WIN0 = (0, 0, 128, 256)
-OFF = (0, 104, 80, 56)
 COLS = ((0, 512), (512, 512), (1024, 640))
 UPB = ((0, 512), (512, 512), (1024, 512), (1536, 512))
 NB = len(COLS)
@@ -30,8 +27,8 @@
 
 def kernel(x_hbm, lns_ref, wq_hbm, wk_hbm, wv_hbm, qs_ref, ks_ref, wo_hbm, bo_ref, wu_hbm, bu_ref, wd_hbm, bd_ref,
            out_hbm,
-           x_s, wq_s, wk_s, wv_s, wo_s, wu_s, wd_s,
-           h_s, proj_s, q4_s, k4_s, v4_s, o_s, act_s, acc_s,
+           x_s, wt_s, wo_s, wu_s, wd_s,
+           h_s, ot_s, q4_s, k4_s, v4_s, o_s, act_s, acc_s,
            dsend, drecv, xsend, xrecv, y_s,
            wsem, iosem, dss, drs, xss, xrs, fss, frs):
     tp = lax.axis_index("tp")
@@ -49,9 +46,9 @@
         nsem[0] += 1
 
     for l in range(2):
-        wcopy("k", l, wk_hbm.at[l], wk_s.at[l])
-        wcopy("v", l, wv_hbm.at[l], wv_s.at[l])
-        wcopy("q", l, wq_hbm.at[l], wq_s.at[l])
+        wcopy("k", l, wk_hbm.at[l], wt_s.at[l, pl.ds(0, HW)])
+        wcopy("v", l, wv_hbm.at[l], wt_s.at[l, pl.ds(HW, HW)])
+        wcopy("q", l, wq_hbm.at[l], wt_s.at[l, pl.ds(2 * HW, HW)])
         for i, (n0, nn) in enumerate(UPB):
             wcopy(("u", i), l, wu_hbm.at[l, :, pl.ds(n0, nn)], wu_s.at[l, :, pl.ds(n0, nn)])
         for i, (n0, nn) in enumerate(COLS):
@@ -71,18 +68,11 @@
     for peer in (sib, cross):
         pl.semaphore_signal(barrier, inc=1, device_id={"tp": peer}, device_id_type=MESH)
 
-    lane = lax.broadcasted_iota(jnp.int32, (8, WIN), 1)
-    masks = [(lane >= OFF[i]) & (lane < OFF[i] + HD) for i in range(NH)]
-
-    def mask_of(i, rows):
-        lane_r = lax.broadcasted_iota(jnp.int32, (rows, WIN), 1)
-        return (lane_r >= OFF[i]) & (lane_r < OFF[i] + HD)
-
-    def gain_windows(ref, l):
+    def gain_cols(ref, l):
         g = ref[l : l + 1, :].astype(F32)
-        g = jnp.concatenate([g, jnp.zeros((1, WIN - HD), F32)], axis=1)
-        g8 = jnp.broadcast_to(g, (8, WIN))
-        return [(pltpu.roll(g8, OFF[i], 1) if OFF[i] else g8)[0:1, :] for i in range(NH)]
+        g = jnp.concatenate([g, jnp.zeros((1, 128 - HD), F32)], axis=1)
+        g = jnp.broadcast_to(g, (128, 128)).T[0:HD, :]
+        return jnp.concatenate([g, g], axis=1)
 
     def ln_rows(src, l, rows):
         v = src[rows, :].astype(F32)
@@ -92,50 +82,39 @@
         g = lns_ref[l : l + 1, :].astype(F32)
         h_s[rows, :] = (cen * lax.rsqrt(var + LN_EPS) * g).astype(BF16)
 
-    def head_norm(dst, gains, rows, n):
+    def project(l, r0, rows):
+        return lax.dot_general(wt_s[l, pl.ds(r0, HW), :], h_s[rows, :], (((1,), (1,)), ((), ())), preferred_element_type=F32)
+
+    def head_norm(dst, pt, gains, rows, n):
         for i in range(NH):
-            w = proj_s[rows, pl.ds(WIN0[i], WIN)]
-            m = mask_of(i, n)
-            w = jnp.where(m, w, 0.0)
-            mean = jnp.sum(w, axis=1, keepdims=True) * (1.0 / HD)
-            cen = jnp.where(m, w - mean, 0.0)
-            var = jnp.sum(cen * cen, axis=1, keepdims=True) * (1.0 / HD)
-            dst[i, rows, :] = (cen * lax.rsqrt(var + LN_EPS) * gains[i]).astype(BF16)
-
-    def project(w_s, l, rows):
-        proj_s[rows, pl.ds(0, HW)] = jnp.dot(h_s[rows, :], w_s[l], preferred_element_type=F32)
+            w = pt[i * HD : (i + 1) * HD, :]
+            mean = jnp.sum(w, axis=0, keepdims=True) * (1.0 / HD)
+            cen = w - mean
+            var = jnp.sum(cen * cen, axis=0, keepdims=True) * (1.0 / HD)
+            dst[i, :, rows] = (cen * lax.rsqrt(var + LN_EPS) * gains[:, 0:n]).astype(BF16)
 
     def do_k(l, rows, n, gk):
         need("k", l)
-        project(wk_s, l, rows)
-        head_norm(k4_s, gk, rows, n)
+        head_norm(k4_s, project(l, 0, rows), gk, rows, n)
 
     def do_v(l, rows, n):
         need("v", l)
-        project(wv_s, l, rows)
+        pt = project(l, HW, rows)
         for i in range(NH):
-            w = proj_s[rows, pl.ds(WIN0[i], WIN)]
-            v4_s[i, rows, :] = jnp.where(mask_of(i, n), w, 0.0).astype(BF16)
+            v4_s[i, :, rows] = pt[i * HD : (i + 1) * HD, :].astype(BF16)
 
     def do_q(l, rows, n, gq):
         need("q", l)
-        project(wq_s, l, rows)
-        head_norm(q4_s, gq, rows, n)
+        head_norm(q4_s, project(l, 2 * HW, rows), gq, rows, n)
 
     def attend(rows):
-        os = []
         for i in range(NH):
-            s = lax.dot_general(q4_s[i, rows, :], k4_s[i], (((1,), (1,)), ((), ())), preferred_element_type=F32)
+            s = lax.dot_general(k4_s[i], q4_s[i, :, rows], (((0,), (0,)), ((), ())), preferred_element_type=F32)
             s = s * (HD ** -0.5)
-            e = jnp.exp(s - jnp.max(s, axis=1, keepdims=True))
-            p = (e * (1.0 / jnp.sum(e, axis=1, keepdims=True))).astype(BF16)
-            os.append(jnp.dot(p, v4_s[i], preferred_element_type=F32))
-        lo = [o[:, 0:128] for o in os]
-        hi = [o[:, 128:256] for o in os]
-        o_s[rows, 0:128] = (lo[0] + lo[1]).astype(BF16)
-        o_s[rows, 128:256] = (hi[1] + lo[2]).astype(BF16)
-        o_s[rows, 256:384] = (hi[2] + lo[3]).astype(BF16)
-        o_s[rows, 384:512] = hi[3].astype(BF16)
+            e = jnp.exp(s - jnp.max(s, axis=0, keepdims=True))
+            p = (e * (1.0 / jnp.sum(e, axis=0, keepdims=True))).astype(BF16)
+            ot_s[pl.ds(i * HD, HD), :] = jnp.dot(v4_s[i], p, preferred_element_type=F32)
+        o_s[rows, :] = ot_s[...].T.astype(BF16)
 
     def do_up(l, rows):
         for i, (n0, nn) in enumerate(UPB):
@@ -201,16 +180,16 @@
         f_rdma(l, c, b).start()
 
     rows = [pl.ds(0, CH), pl.ds(CH, CH)]
-    proj_s[:, pl.ds(HW, 512 - HW)] = jnp.zeros((T, 512 - HW), F32)
-
-    gk = gain_windows(ks_ref, 0)
-    gq = gain_windows(qs_ref, 0)
+    ot_s[pl.ds(HW, 512 - HW), :] = jnp.zeros((512 - HW, CH), F32)
+
+    gk = gain_cols(ks_ref, 0)
+    gq = gain_cols(qs_ref, 0)
     xcopy.wait()
     ln_rows(x_s, 0, rows[0])
     ln_rows(x_s, 0, rows[1])
     do_k(0, pl.ds(0, T), T, gk)
     do_v(0, pl.ds(0, T), T)
-    do_q(0, rows[0], CH, gq)
+    do_q(0, pl.ds(0, T), T, gq)
     attend(rows[0])
     do_up(0, rows[0])
     pl.semaphore_wait(barrier, 2)
@@ -221,7 +200,6 @@
     for (name, l), cp in wcopies.items():
         if l == 1:
             cp.start()
-    do_q(0, rows[1], CH, gq)
     cross_block(0, 0, NB - 1)
     attend(rows[1])
     do_up(0, rows[1])
@@ -229,8 +207,8 @@
         emit_block(0, 1, b, mlp_block(0, 1, rows[1], b) + attn_block(0, 1, rows[1], b))
         if b >= 1:
             cross_block(0, 1, b - 1)
-    gk = gain_windows(ks_ref, 1)
-    gq = gain_windows(qs_ref, 1)
+    gk = gain_cols(ks_ref, 1)
+    gq = gain_cols(qs_ref, 1)
     cross_block(0, 1, NB - 1)
 
     for b in range(NB):
@@ -307,17 +285,15 @@
         out_specs=any_spec,
         scratch_shapes=[
             pltpu.VMEM((T, D), BF16),
-            pltpu.VMEM((2, D, HW), BF16),
-            pltpu.VMEM((2, D, HW), BF16),
-            pltpu.VMEM((2, D, HW), BF16),
+            pltpu.VMEM((2, 3 * HW, D), BF16),
             pltpu.VMEM((2, HW, D), BF16),
             pltpu.VMEM((2, D, FF), BF16),
             pltpu.VMEM((2, FF, D), BF16),
             pltpu.VMEM((T, D), BF16),
-            pltpu.VMEM((T, 512), F32),
-            pltpu.VMEM((NH, T, WIN), BF16),
-            pltpu.VMEM((NH, T, WIN), BF16),
-            pltpu.VMEM((NH, T, WIN), BF16),
+            pltpu.VMEM((512, CH), F32),
+            pltpu.VMEM((NH, HD, T), BF16),
+            pltpu.VMEM((NH, HD, T), BF16),
+            pltpu.VMEM((NH, HD, T), BF16),
             pltpu.VMEM((T, 512), BF16),
             pltpu.VMEM((T, FF), BF16),
             pltpu.VMEM((2, CH, D), F32),
@@ -339,7 +315,7 @@
         name="vit_pair",
     )
 
-    def per_device(*args):
-        return call(*args)
+    def per_device(x, lns, wq, wk, wv, *rest):
+        return call(x, lns, *(jnp.swapaxes(w, 1, 2) for w in (wq, wk, wv)), *rest)
 
     return jax.shard_map(per_device, mesh=mesh, in_specs=in_specs, out_specs=P("dp", None, None), check_vma=False)

time: 68.1 us -> 52.6 us (0.77)
  local copies, waits for them, and re-layouts: 16.6 us -> 2.12 us
  Pallas kernels: 51.1 us -> 50.3 us
    unnamed x6 -> x1, local copies, waits for them, and re-layouts: 16.6 us -> 2.12 us
    pallas_call x1, Pallas kernels: 51.1 us -> 50.3 us  [per_device(): return call(x, lns, *(jnp.swapaxes(w, 1, 2) for w in (wq, wk, wv)), *rest)]
where the time goes in v2:
time: 52.6 us; the launch traced here: 52.4 us
  Pallas kernels  50.3 us (96%)
  local copies, waits for them, and re-layouts  2.12 us (4%)
    pallas_call x1, Pallas kernels, per_device(): return call(x, lns, *(jnp.swapaxes(w, 1, 2) for w in (wq, wk, wv)), *rest)  50.3 us
    unnamed x1, local copies, waits for them, and re-layouts  2.12 us

profile of v2, /device:TPU:0, one launch (start us, length us, event | category | flops | bytes accessed | tf_op | source)
XLA Modules:
  0.0 52.4 jit_solution(18349531633469895251)
XLA Ops:
  0.0 50.3 %vit_pair.1 = bf16[1,256,1664]{2,1,0:T(8,128)(2,1)} custom-call(bf16[1,256,1664]{2,1,0:T(8,128)(2,1)} %x_hbm.1, bf16[2,1664]{1,0:T(2,128)(2,1)} %lns_ref.1, bf16[2,416,1664]{2,1,0:T(8,128)(2,1)} %bitcast.3, bf16[2,416,1664]{2,1,0:T(8,128)(2,1)} %bitcast.4, bf16[2,416,1664]{2,1,0:T(8,128)(2,1)} %bitcast.5, bf16[2,104]{1,0:T(2,128)(2,1)} %qs_ref.1, ...), custom_call_target="tpu_custom_call" | custom-call | tf_op jit(solution)/shard_map/vit_pair/pallas_call | solution.py:319
  50.3 2.1 %copy.15 = bf16[1,256,1664]{2,1,0:T(8,128)(2,1)} copy(bf16[1,256,1664]{2,1,0:T(8,128)(2,1)} %vit_pair.1) | data formatting | bytes 1703936

commit v3 on v2

--- a/solution.py
+++ b/solution.py
@@ -25,9 +25,9 @@
 NB = len(COLS)
 
 
-def kernel(x_hbm, lns_ref, wq_hbm, wk_hbm, wv_hbm, qs_ref, ks_ref, wo_hbm, bo_ref, wu_hbm, bu_ref, wd_hbm, bd_ref,
-           out_hbm,
-           x_s, wt_s, wo_s, wu_s, wd_s,
+def kernel(x_hbm, lns_hbm, wq_hbm, wk_hbm, wv_hbm, qs_hbm, ks_hbm, wo_hbm, bo_hbm, wu_hbm, bu_hbm, wd_hbm, bd_hbm,
+           out_ref,
+           lns_ref, qs_ref, ks_ref, bo_ref, bu_ref, bd_ref, x_s, wt_s, wo_s, wu_s, wd_s,
            h_s, ot_s, q4_s, k4_s, v4_s, o_s, act_s, acc_s,
            dsend, drecv, xsend, xrecv, y_s,
            wsem, iosem, dss, drs, xss, xrs, fss, frs):
@@ -38,6 +38,16 @@
 
     xcopy = pltpu.make_async_copy(x_hbm.at[0], x_s, iosem.at[0])
     xcopy.start()
+    smalls = [
+        pltpu.make_async_copy(src, dst, iosem.at[1 + i])
+        for i, (src, dst) in enumerate(
+            ((lns_hbm, lns_ref), (ks_hbm, ks_ref), (qs_hbm, qs_ref), (bu_hbm, bu_ref), (bo_hbm, bo_ref), (bd_hbm, bd_ref)))
+    ]
+    for cp in smalls:
+        cp.start()
+    barrier = pltpu.get_barrier_semaphore()
+    for peer in (sib, cross):
+        pl.semaphore_signal(barrier, inc=1, device_id={"tp": peer}, device_id_type=MESH)
     wcopies = {}
     nsem = [0]
 
@@ -64,10 +74,6 @@
             waited.add((name, l))
             wcopies[(name, l)].wait()
 
-    barrier = pltpu.get_barrier_semaphore()
-    for peer in (sib, cross):
-        pl.semaphore_signal(barrier, inc=1, device_id={"tp": peer}, device_id_type=MESH)
-
     def gain_cols(ref, l):
         g = ref[l : l + 1, :].astype(F32)
         g = jnp.concatenate([g, jnp.zeros((1, 128 - HD), F32)], axis=1)
@@ -82,30 +88,43 @@
         g = lns_ref[l : l + 1, :].astype(F32)
         h_s[rows, :] = (cen * lax.rsqrt(var + LN_EPS) * g).astype(BF16)
 
-    def project(l, r0, rows):
-        return lax.dot_general(wt_s[l, pl.ds(r0, HW), :], h_s[rows, :], (((1,), (1,)), ((), ())), preferred_element_type=F32)
-
-    def head_norm(dst, pt, gains, rows, n):
-        for i in range(NH):
-            w = pt[i * HD : (i + 1) * HD, :]
-            mean = jnp.sum(w, axis=0, keepdims=True) * (1.0 / HD)
-            cen = w - mean
-            var = jnp.sum(cen * cen, axis=0, keepdims=True) * (1.0 / HD)
-            dst[i, :, rows] = (cen * lax.rsqrt(var + LN_EPS) * gains[:, 0:n]).astype(BF16)
-
-    def do_k(l, rows, n, gk):
-        need("k", l)
-        head_norm(k4_s, project(l, 0, rows), gk, rows, n)
-
-    def do_v(l, rows, n):
-        need("v", l)
-        pt = project(l, HW, rows)
-        for i in range(NH):
-            v4_s[i, :, rows] = pt[i * HD : (i + 1) * HD, :].astype(BF16)
-
-    def do_q(l, rows, n, gq):
+    def project(l, r0, nr, rows):
+        return lax.dot_general(wt_s[l, pl.ds(r0, nr), :], h_s[rows, :], (((1,), (1,)), ((), ())), preferred_element_type=F32)
+
+    def head_norm(dst, i, w, gains, rows, n):
+        mean = jnp.sum(w, axis=0, keepdims=True) * (1.0 / HD)
+        cen = w - mean
+        var = jnp.sum(cen * cen, axis=0, keepdims=True) * (1.0 / HD)
+        dst[i, :, rows] = (cen * lax.rsqrt(var + LN_EPS) * gains[:, 0:n]).astype(BF16)
+
+    def place(kind, i, w, l, rows, n):
+        if kind == 0:
+            head_norm(k4_s, i, w, gain_cols(ks_ref, l), rows, n)
+        elif kind == 1:
+            v4_s[i, :, rows] = w.astype(BF16)
+        else:
+            head_norm(q4_s, i, w, gain_cols(qs_ref, l), rows, n)
+
+    def heads(l, r0, nr, rows, n):
+        half = nr // 2
+        parts = [project(l, r0, half, rows), project(l, r0 + half, half, rows)]
+        for g in range(r0 // HD, (r0 + nr) // HD):
+            p, off = divmod(g * HD - r0, half)
+            place(g // NH, g % NH, parts[p][off : off + HD, :], l, rows, n)
+
+    def do_kvq(l, rows, n):
+        for name in "kvq":
+            need(name, l)
+        heads(l, 0, 3 * HW, rows, n)
+
+    def do_kv(l, rows, n):
+        for name in "kv":
+            need(name, l)
+        heads(l, 0, 2 * HW, rows, n)
+
+    def do_q(l, rows, n):
         need("q", l)
-        head_norm(q4_s, project(l, 2 * HW, rows), gq, rows, n)
+        heads(l, 2 * HW, HW, rows, n)
 
     def attend(rows):
         for i in range(NH):
@@ -176,20 +195,21 @@
         res = x_s[r, pl.ds(n0, nn)] if l == 0 else y_s[0, r, pl.ds(n0, nn)]
         base = res.astype(F32) + bo_ref[l : l + 1, pl.ds(n0, nn)].astype(F32) + bd_ref[l : l + 1, pl.ds(n0, nn)].astype(F32)
         both = xsend[l, c, :, pl.ds(n0, nn)].astype(F32) + xrecv[l, c, :, pl.ds(n0, nn)].astype(F32)
-        y_s[l, r, pl.ds(n0, nn)] = (base + both).astype(BF16)
+        y = (base + both).astype(BF16)
+        y_s[l, r, pl.ds(n0, nn)] = y
+        if l == 1:
+            out_ref[0, r, pl.ds(n0, nn)] = y
         f_rdma(l, c, b).start()
 
     rows = [pl.ds(0, CH), pl.ds(CH, CH)]
     ot_s[pl.ds(HW, 512 - HW), :] = jnp.zeros((512 - HW, CH), F32)
 
-    gk = gain_cols(ks_ref, 0)
-    gq = gain_cols(qs_ref, 0)
     xcopy.wait()
+    for cp in smalls:
+        cp.wait()
     ln_rows(x_s, 0, rows[0])
     ln_rows(x_s, 0, rows[1])
-    do_k(0, pl.ds(0, T), T, gk)
-    do_v(0, pl.ds(0, T), T)
-    do_q(0, pl.ds(0, T), T, gq)
+    do_kvq(0, pl.ds(0, T), T)
     attend(rows[0])
     do_up(0, rows[0])
     pl.semaphore_wait(barrier, 2)
@@ -207,8 +227,6 @@
         emit_block(0, 1, b, mlp_block(0, 1, rows[1], b) + attn_block(0, 1, rows[1], b))
         if b >= 1:
             cross_block(0, 1, b - 1)
-    gk = gain_cols(ks_ref, 1)
-    gq = gain_cols(qs_ref, 1)
     cross_block(0, 1, NB - 1)
 
     for b in range(NB):
@@ -217,9 +235,7 @@
         f_rdma(0, 0, b).wait_recv()
     y0 = y_s.at[0]
     ln_rows(y0, 1, rows[0])
-    do_k(1, rows[0], CH, gk)
-    do_v(1, rows[0], CH)
-    do_q(1, rows[0], CH, gq)
+    do_kvq(1, rows[0], CH)
     do_up(1, rows[0])
     for b in range(NB):
         acc_s[0, :, pl.ds(*COLS[b])] = mlp_block(1, 0, rows[0], b)
@@ -228,14 +244,13 @@
     for b in range(NB):
         f_rdma(0, 1, b).wait_recv()
     ln_rows(y0, 1, rows[1])
-    do_k(1, rows[1], CH, gk)
-    do_v(1, rows[1], CH)
+    do_kv(1, rows[1], CH)
     attend(rows[0])
     for b in range(NB):
         emit_block(1, 0, b, acc_s[0, :, pl.ds(*COLS[b])] + attn_block(1, 0, rows[0], b))
         if b >= 1:
             cross_block(1, 0, b - 1)
-    do_q(1, rows[1], CH, gq)
+    do_q(1, rows[1], CH)
     cross_block(1, 0, NB - 1)
     attend(rows[1])
     do_up(1, rows[1])
@@ -245,30 +260,20 @@
             cross_block(1, 1, b - 1)
     cross_block(1, 1, NB - 1)
 
-    def out_own(c):
-        r = pl.ds(pl.multiple_of(c * CH + core * OWN, OWN), OWN)
-        return pltpu.make_async_copy(y_s.at[1, r], out_hbm.at[0, r], iosem.at[1 + 2 * c])
-
-    def out_sib(c):
-        r = pl.ds(pl.multiple_of(c * CH + (1 - core) * OWN, OWN), OWN)
-        return pltpu.make_async_copy(y_s.at[1, r], out_hbm.at[0, r], iosem.at[2 + 2 * c])
-
     for c in range(2):
         for b in range(NB):
             finish_block(1, c, b)
-        out_own(c).start()
         for b in range(NB):
+            n0, nn = COLS[b]
             f_rdma(1, c, b).wait_recv()
-        out_sib(c).start()
+            r = pl.ds(pl.multiple_of(c * CH + (1 - core) * OWN, OWN), OWN)
+            out_ref[0, r, pl.ds(n0, nn)] = y_s[1, r, pl.ds(n0, nn)]
     for l in range(2):
         for c in range(2):
             for b in range(NB):
                 d_rdma(l, c, b).wait_send()
                 x_rdma(l, c, b).wait_send()
                 f_rdma(l, c, b).wait_send()
-    for c in range(2):
-        out_own(c).wait()
-        out_sib(c).wait()
 
 
 def solution(mesh):
@@ -280,10 +285,16 @@
     nw = 2 * (3 + len(UPB) + 2 * NB)
     call = pl.pallas_call(
         kernel,
-        out_shape=jax.ShapeDtypeStruct((1, T, D), BF16),
-        in_specs=[any_spec, vmem_spec, any_spec, any_spec, any_spec, vmem_spec, vmem_spec, any_spec, vmem_spec, any_spec, vmem_spec, any_spec, vmem_spec],
-        out_specs=any_spec,
+        out_shape=pltpu.VMEM((1, T, D), BF16),
+        in_specs=[any_spec] * 13,
+        out_specs=vmem_spec,
         scratch_shapes=[
+            pltpu.VMEM((2, D), BF16),
+            pltpu.VMEM((2, HD), BF16),
+            pltpu.VMEM((2, HD), BF16),
+            pltpu.VMEM((2, D), BF16),
+            pltpu.VMEM((2, FF), BF16),
+            pltpu.VMEM((2, D), BF16),
             pltpu.VMEM((T, D), BF16),
             pltpu.VMEM((2, 3 * HW, D), BF16),
             pltpu.VMEM((2, HW, D), BF16),
@@ -303,7 +314,7 @@
             pltpu.VMEM((2, 2, OWN, D), BF16),
             pltpu.VMEM((2, T, D), BF16),
             pltpu.SemaphoreType.DMA((nw,)),
-            pltpu.SemaphoreType.DMA((5,)),
+            pltpu.SemaphoreType.DMA((7,)),
             pltpu.SemaphoreType.DMA((2, 2, NB)),
             pltpu.SemaphoreType.DMA((2, 2, NB)),
             pltpu.SemaphoreType.DMA((2, 2, NB)),
@@ -311,7 +322,7 @@
             pltpu.SemaphoreType.DMA((2, 2, NB)),
             pltpu.SemaphoreType.DMA((2, 2, NB)),
         ],
-        compiler_params=pltpu.CompilerParams(collective_id=0, has_side_effects=True, vmem_limit_bytes=62 * 1024 * 1024),
+        compiler_params=pltpu.CompilerParams(collective_id=0, has_side_effects=True, vmem_limit_bytes=54 * 1024 * 1024),
         name="vit_pair",
     )
 

time: 52.6 us -> 44.2 us (0.84)
  Pallas kernels: 50.3 us -> 43.2 us
  local copies, waits for them, and re-layouts: 2.12 us -> 0.9 us
    pallas_call x1, Pallas kernels: 50.3 us -> 43.2 us  [per_device(): return call(x, lns, *(jnp.swapaxes(w, 1, 2) for w in (wq, wk, wv)), *rest)]
    unnamed x1, local copies, waits for them, and re-layouts: 2.12 us -> 0.9 us
where the time goes in v3:
time: 44.2 us; the launch traced here: 44.1 us
  Pallas kernels  43.2 us (98%)
  local copies, waits for them, and re-layouts  0.9 us (2%)
    pallas_call x1, Pallas kernels, per_device(): return call(x, lns, *(jnp.swapaxes(w, 1, 2) for w in (wq, wk, wv)), *rest)  43.2 us
    unnamed x1, local copies, waits for them, and re-layouts  0.9 us

profile of v3, /device:TPU:0, one launch (start us, length us, event | category | flops | bytes accessed | tf_op | source)
XLA Modules:
  0.0 44.1 jit_solution(18247178454932291663)
XLA Ops:
  0.0 43.2 %vit_pair.1 = bf16[1,256,1664]{2,1,0:T(8,128)(2,1)S(1)} custom-call(bf16[1,256,1664]{2,1,0:T(8,128)(2,1)} %x_hbm.1, bf16[2,1664]{1,0:T(2,128)(2,1)} %lns_hbm.1, bf16[2,416,1664]{2,1,0:T(8,128)(2,1)} %bitcast.3, bf16[2,416,1664]{2,1,0:T(8,128)(2,1)} %bitcast.4, bf16[2,416,1664]{2,1,0:T(8,128)(2,1)} %bitcast.5, bf16[2,104]{1,0:T(2,128)(2,1)} %qs_hbm.1, ...), custom_call_target="tpu_custom_call" | custom-call | tf_op jit(solution)/shard_map/vit_pair/pallas_call | solution.py:330
  43.2 0.9 %copy.15 = bf16[1,256,1664]{2,1,0:T(8,128)(2,1)} copy(bf16[1,256,1664]{2,1,0:T(8,128)(2,1)S(1)} %vit_pair.1) | data formatting | bytes 1703936

commit v4 on v3

--- a/solution.py
+++ b/solution.py
@@ -28,7 +28,7 @@
 def kernel(x_hbm, lns_hbm, wq_hbm, wk_hbm, wv_hbm, qs_hbm, ks_hbm, wo_hbm, bo_hbm, wu_hbm, bu_hbm, wd_hbm, bd_hbm,
            out_ref,
            lns_ref, qs_ref, ks_ref, bo_ref, bu_ref, bd_ref, x_s, wt_s, wo_s, wu_s, wd_s,
-           h_s, ot_s, q4_s, k4_s, v4_s, o_s, act_s, acc_s,
+           h_s, ot_s, s_s, p_s, q4_s, k4_s, v4_s, o_s, act_s, acc_s,
            dsend, drecv, xsend, xrecv, y_s,
            wsem, iosem, dss, drs, xss, xrs, fss, frs):
     tp = lax.axis_index("tp")
@@ -57,8 +57,8 @@
 
     for l in range(2):
         wcopy("k", l, wk_hbm.at[l], wt_s.at[l, pl.ds(0, HW)])
+        wcopy("q", l, wq_hbm.at[l], wt_s.at[l, pl.ds(2 * HW, HW)])
         wcopy("v", l, wv_hbm.at[l], wt_s.at[l, pl.ds(HW, HW)])
-        wcopy("q", l, wq_hbm.at[l], wt_s.at[l, pl.ds(2 * HW, HW)])
         for i, (n0, nn) in enumerate(UPB):
             wcopy(("u", i), l, wu_hbm.at[l, :, pl.ds(n0, nn)], wu_s.at[l, :, pl.ds(n0, nn)])
         for i, (n0, nn) in enumerate(COLS):
@@ -91,48 +91,40 @@
     def project(l, r0, nr, rows):
         return lax.dot_general(wt_s[l, pl.ds(r0, nr), :], h_s[rows, :], (((1,), (1,)), ((), ())), preferred_element_type=F32)
 
-    def head_norm(dst, i, w, gains, rows, n):
+    def head_norm(w, gains, n):
         mean = jnp.sum(w, axis=0, keepdims=True) * (1.0 / HD)
         cen = w - mean
         var = jnp.sum(cen * cen, axis=0, keepdims=True) * (1.0 / HD)
-        dst[i, :, rows] = (cen * lax.rsqrt(var + LN_EPS) * gains[:, 0:n]).astype(BF16)
-
-    def place(kind, i, w, l, rows, n):
-        if kind == 0:
-            head_norm(k4_s, i, w, gain_cols(ks_ref, l), rows, n)
-        elif kind == 1:
-            v4_s[i, :, rows] = w.astype(BF16)
-        else:
-            head_norm(q4_s, i, w, gain_cols(qs_ref, l), rows, n)
-
-    def heads(l, r0, nr, rows, n):
-        half = nr // 2
-        parts = [project(l, r0, half, rows), project(l, r0 + half, half, rows)]
-        for g in range(r0 // HD, (r0 + nr) // HD):
-            p, off = divmod(g * HD - r0, half)
-            place(g // NH, g % NH, parts[p][off : off + HD, :], l, rows, n)
-
-    def do_kvq(l, rows, n):
-        for name in "kvq":
-            need(name, l)
-        heads(l, 0, 3 * HW, rows, n)
-
-    def do_kv(l, rows, n):
-        for name in "kv":
-            need(name, l)
-        heads(l, 0, 2 * HW, rows, n)
-
-    def do_q(l, rows, n):
-        need("q", l)
-        heads(l, 2 * HW, HW, rows, n)
-
-    def attend(rows):
+        normed = cen * lax.rsqrt(var + LN_EPS) * gains[:, 0:n]
+        return jnp.concatenate([normed, jnp.zeros((128 - HD, n), F32)], axis=0)
+
+    def heads(l, kind, rows, n):
+        need("kvq"[kind], l)
+        half = HW // 2
+        parts = [project(l, kind * HW, half, rows), project(l, kind * HW + half, half, rows)]
+        if kind != 1:
+            gains = gain_cols(ks_ref if kind == 0 else qs_ref, l)
         for i in range(NH):
-            s = lax.dot_general(k4_s[i], q4_s[i, :, rows], (((0,), (0,)), ((), ())), preferred_element_type=F32)
-            s = s * (HD ** -0.5)
+            p, off = divmod(i * HD, half)
+            w = parts[p][off : off + HD, :]
+            if kind == 0:
+                k4_s[i, rows, :] = head_norm(w, gains, n).T.astype(BF16)
+            elif kind == 1:
+                v4_s[i, :, rows] = w.astype(BF16)
+            else:
+                q4_s[i, :, rows] = head_norm(w, gains, n).astype(BF16)
+
+    def scores(rows, keys):
+        for i in range(NH):
+            s_s[i, keys, :] = jnp.dot(k4_s[i, keys, :], q4_s[i, :, rows], preferred_element_type=F32)
+
+    def mix(rows):
+        for i in range(NH):
+            s = s_s[i] * (HD ** -0.5)
             e = jnp.exp(s - jnp.max(s, axis=0, keepdims=True))
-            p = (e * (1.0 / jnp.sum(e, axis=0, keepdims=True))).astype(BF16)
-            ot_s[pl.ds(i * HD, HD), :] = jnp.dot(v4_s[i], p, preferred_element_type=F32)
+            p_s[i] = (e * (1.0 / jnp.sum(e, axis=0, keepdims=True))).astype(BF16)
+        for i in range(NH):
+            ot_s[pl.ds(i * HD, HD), :] = jnp.dot(v4_s[i], p_s[i], preferred_element_type=F32)
         o_s[rows, :] = ot_s[...].T.astype(BF16)
 
     def do_up(l, rows):
@@ -209,8 +201,12 @@
         cp.wait()
     ln_rows(x_s, 0, rows[0])
     ln_rows(x_s, 0, rows[1])
-    do_kvq(0, pl.ds(0, T), T)
-    attend(rows[0])
+    every = pl.ds(0, T)
+    heads(0, 0, every, T)
+    heads(0, 2, every, T)
+    scores(rows[0], every)
+    heads(0, 1, every, T)
+    mix(rows[0])
     do_up(0, rows[0])
     pl.semaphore_wait(barrier, 2)
     for b in range(NB):
@@ -220,8 +216,9 @@
     for (name, l), cp in wcopies.items():
         if l == 1:
             cp.start()
+    scores(rows[1], every)
     cross_block(0, 0, NB - 1)
-    attend(rows[1])
+    mix(rows[1])
     do_up(0, rows[1])
     for b in range(NB):
         emit_block(0, 1, b, mlp_block(0, 1, rows[1], b) + attn_block(0, 1, rows[1], b))
@@ -235,7 +232,9 @@
         f_rdma(0, 0, b).wait_recv()
     y0 = y_s.at[0]
     ln_rows(y0, 1, rows[0])
-    do_kvq(1, rows[0], CH)
+    for kind in range(3):
+        heads(1, kind, rows[0], CH)
+    scores(rows[0], rows[0])
     do_up(1, rows[0])
     for b in range(NB):
         acc_s[0, :, pl.ds(*COLS[b])] = mlp_block(1, 0, rows[0], b)
@@ -244,15 +243,18 @@
     for b in range(NB):
         f_rdma(0, 1, b).wait_recv()
     ln_rows(y0, 1, rows[1])
-    do_kv(1, rows[1], CH)
-    attend(rows[0])
+    heads(1, 0, rows[1], CH)
+    scores(rows[0], rows[1])
+    heads(1, 1, rows[1], CH)
+    mix(rows[0])
     for b in range(NB):
         emit_block(1, 0, b, acc_s[0, :, pl.ds(*COLS[b])] + attn_block(1, 0, rows[0], b))
         if b >= 1:
             cross_block(1, 0, b - 1)
-    do_q(1, rows[1], CH)
+    heads(1, 2, rows[1], CH)
+    scores(rows[1], every)
     cross_block(1, 0, NB - 1)
-    attend(rows[1])
+    mix(rows[1])
     do_up(1, rows[1])
     for b in range(NB):
         emit_block(1, 1, b, mlp_block(1, 1, rows[1], b) + attn_block(1, 1, rows[1], b))
@@ -302,8 +304,10 @@
             pltpu.VMEM((2, FF, D), BF16),
             pltpu.VMEM((T, D), BF16),
             pltpu.VMEM((512, CH), F32),
-            pltpu.VMEM((NH, HD, T), BF16),
-            pltpu.VMEM((NH, HD, T), BF16),
+            pltpu.VMEM((NH, T, CH), F32),
+            pltpu.VMEM((NH, T, CH), BF16),
+            pltpu.VMEM((NH, 128, T), BF16),
+            pltpu.VMEM((NH, T, 128), BF16),
             pltpu.VMEM((NH, HD, T), BF16),
             pltpu.VMEM((T, 512), BF16),
             pltpu.VMEM((T, FF), BF16),

time: 44.2 us -> 42.6 us (0.964)
  Pallas kernels: 43.2 us -> 41.6 us
    pallas_call x1, Pallas kernels: 43.2 us -> 41.6 us  [per_device(): return call(x, lns, *(jnp.swapaxes(w, 1, 2) for w in (wq, wk, wv)), *rest)]
where the time goes in v4:
time: 42.6 us; the launch traced here: 42.5 us
  Pallas kernels  41.6 us (98%)
  local copies, waits for them, and re-layouts  0.9 us (2%)
    pallas_call x1, Pallas kernels, per_device(): return call(x, lns, *(jnp.swapaxes(w, 1, 2) for w in (wq, wk, wv)), *rest)  41.6 us
    unnamed x1, local copies, waits for them, and re-layouts  0.9 us

profile of v4, /device:TPU:0, one launch (start us, length us, event | category | flops | bytes accessed | tf_op | source)
XLA Modules:
  0.0 42.5 jit_solution(4186214074022754159)
XLA Ops:
  0.0 41.6 %vit_pair.1 = bf16[1,256,1664]{2,1,0:T(8,128)(2,1)S(1)} custom-call(bf16[1,256,1664]{2,1,0:T(8,128)(2,1)} %x_hbm.1, bf16[2,1664]{1,0:T(2,128)(2,1)} %lns_hbm.1, bf16[2,416,1664]{2,1,0:T(8,128)(2,1)} %bitcast.3, bf16[2,416,1664]{2,1,0:T(8,128)(2,1)} %bitcast.4, bf16[2,416,1664]{2,1,0:T(8,128)(2,1)} %bitcast.5, bf16[2,104]{1,0:T(2,128)(2,1)} %qs_hbm.1, ...), custom_call_target="tpu_custom_call" | custom-call | tf_op jit(solution)/shard_map/vit_pair/pallas_call | solution.py:334
  41.6 0.9 %copy.15 = bf16[1,256,1664]{2,1,0:T(8,128)(2,1)} copy(bf16[1,256,1664]{2,1,0:T(8,128)(2,1)S(1)} %vit_pair.1) | data formatting | bytes 1703936
